TPU v7x, 128 devices: a 2x2x16 block of a 8x8x16 slice. The times are simulated.
128 devices in a mesh: member: 4 (over x, y), gx: 32 (over z, core).
Axes of the slice: x: 2, y: 2, z: 16, core: 2. Of those that a mesh axis runs over, the one named last changes fastest.
The devices are a block of a 8x8x16 slice.
Arguments:
- perturbation: float32 [512, 128, 512], P(('member', 'gx')), parts along dimension 0, may hold values from -6 to 6
- vertical: float32 [512, 128], P('member'), parts along dimension 0, may hold values from -0.5 to 0.5
- kappa: float32 [512, 512], P(('member', 'gx')), parts along dimension 0, may hold values from 2 to 8
- sea_mask: int32 [128, 512], P('gx'), may hold values from 0 to 1
- sweeps: int32 [12], P('member'), parts along dimension 0, may hold values from 4 to 8, as said below
Outputs:
- increment: float32 [512, 128, 512], P('member', 'gx'), parts along dimension 0
There are 4 independent parts, one for each index of `member`. A program takes and returns all parts, laid end to end along the dimension named above; an argument that names none is the same for every part. Nothing has to cross between parts.
Inputs may be any that keep to these rules, and one draw needn't show every extreme that they name: `sweeps`: each entry is at least 4, and one of the three entries equals 8.
All inputs are finite; a program needn't handle non-finite values.
Results may differ from a plain program's by a relative error of at most 0.00007.
Values sent between devices are 32-bit elements; how exact they have to be, the bound alone decides.
A program may use at most 64 MiB of HBM per device.

v0:
```python
import jax
import jax.numpy as jnp
from jax import lax
from jax.sharding import PartitionSpec as P

SWEEP_MOST = 8


def sent_to_all(array, axis):
    devices = lax.axis_size(axis)
    return lax.all_to_all(
        jnp.broadcast_to(array[None], (devices, *array.shape)), axis, 0, 0, tiled=True
    )


def joined_along(pieces, dim):
    pieces = jnp.moveaxis(pieces, 0, dim)
    dims = pieces.shape
    return pieces.reshape(*dims[:dim], dims[dim] * dims[dim + 1], *dims[dim + 2 :])


def gathered_copies(array, axis, dim):
    pieces = sent_to_all(array, axis)
    return joined_along(pieces, dim)


def couplings(kpad):
    mpad = jnp.where(kpad > 0.0, 1.0, 0.0).astype(jnp.float32)
    center_k = kpad[1:-1]
    center_m = mpad[1:-1]
    north_side = 0.5 * (center_k + kpad[:-2]) * center_m * mpad[:-2]
    south_side = 0.5 * (center_k + kpad[2:]) * center_m * mpad[2:]
    kwide = jnp.pad(center_k, ((0, 0), (1, 1)))
    mwide = jnp.pad(center_m, ((0, 0), (1, 1)))
    west_side = 0.5 * (center_k + kwide[:, :-2]) * center_m * mwide[:, :-2]
    east_side = 0.5 * (center_k + kwide[:, 2:]) * center_m * mwide[:, 2:]
    denom = 1.0 + north_side + south_side + west_side + east_side
    return (north_side, south_side, west_side, east_side, denom)


def diffuse(field, coefs, sweeps, pad_rows):
    north_side, south_side, west_side, east_side, denom = coefs
    for section in range(3):
        source = field
        count = sweeps[section]

        def sweep(index, iterate):
            rowpad = pad_rows(iterate)
            colpad = jnp.pad(iterate, ((0, 0), (0, 0), (1, 1)))
            gathered = (
                north_side * rowpad[:, :-2]
                + south_side * rowpad[:, 2:]
                + west_side * colpad[:, :, :-2]
                + east_side * colpad[:, :, 2:]
            )
            updated = (source + gathered) / denom
            return jnp.where(index < count, updated, iterate)

        field = lax.fori_loop(0, SWEEP_MOST, sweep, source)
    return field


def zero_rows(iterate):
    return jnp.pad(iterate, ((0, 0), (1, 1), (0, 0)))


def per_device(perturbation, vertical, kappa, sea_mask, sweeps):
    masked = kappa * sea_mask.astype(jnp.float32)
    whole = gathered_copies(masked, "gx", 0)
    padded = jnp.pad(whole, ((1, 1), (0, 0)))
    coefs = couplings(padded)
    smooth = diffuse(perturbation, coefs, sweeps, zero_rows)
    column = lax.all_to_all(smooth, "gx", split_axis=1, concat_axis=0, tiled=True)
    return jnp.einsum("lk,kxy->lxy", vertical, column, precision=lax.Precision.HIGHEST)


def solution(mesh):
    in_specs = (
        P(("member", "gx"), None, None),
        P("member", None),
        P(("member", "gx"), None),
        P("gx", None),
        P("member"),
    )
    out_specs = P("member", "gx", None)
    return jax.shard_map(
        per_device, mesh=mesh, in_specs=in_specs, out_specs=out_specs, check_vma=False
    )
```

profile of v0, /device:TPU:69, one launch (start us, length us, event | category | flops | bytes accessed | tf_op | source)
XLA Modules:
  0.0 165.2 jit_solution(10167537214013671169)
XLA Ops:
  1.5 18.5 %all-to-all-start = ((f32[32,4,512]{2,1,0:T(4,128)}), f32[32,4,512]{2,1,0:T(4,128)S(1)}, u32[]{:S(2)}, u32[]{:S(2)}) async-start(f32[32,4,512]{2,1,0:T(4,128)} %broadcast_in_dim.57), calls=%async_computation | async-start | bytes 524288 | tf_op jit(solution)/shard_map/all_to_all | solution.py:11
  20.0 1.2 copy.18
  21.9 20.2 %all-to-all-done = f32[32,4,512]{2,1,0:T(4,128)S(1)} async-done(((f32[32,4,512]{2,1,0:T(4,128)}), f32[32,4,512]{2,1,0:T(4,128)S(1)}, u32[]{:S(2)}, u32[]{:S(2)}) %all-to-all-start) | async-done | bytes 262176 | tf_op jit(solution)/shard_map/all_to_all | solution.py:11
  43.0 2.0 %add_add_fusion = (f32[128,512]{1,0:T(8,128)S(1)}, f32[128,512]{1,0:T(8,128)S(1)}, f32[128,512]{1,0:T(8,128)S(1)}, f32[128,512]{1,0:T(8,128)S(1)}, f32[128,512]{1,0:T(8,128)S(1)}) fusion(f32[128,512]{1,0:T(8,128)S(1)} %slice.169, f32[128,512]{1,0:T(8,128)} %copy-done.2, f32[130,512]{1,0:T(8,128)S(1)} %compare_select_fusion), kind=kLoop, calls=%fused_computation.59 | loop fusion | flops 1310720 | bytes 2621440 | tf_op jit(solution)/shard_map/add | solution.py:37
  44.9 13.2 %while.45 = (s32[]{:T(128)}, f32[4,128,512]{2,1,0:T(8,128)S(1)}, s32[]{:T(128)}, f32[128,512]{1,0:T(8,128)S(1)}, f32[128,512]{1,0:T(8,128)S(1)}, /*index=5*/f32[...) while((s32[]{:T(128)}, f32[4,128,512]{2,1,0:T(8,128)S(1)}, ...), condition=%wide.region_1.2_spmd, body=%wide.region_0.1_spmd.sunk | while | flops 2621443 | bytes 6553719 | solution.py:59
  58.2 13.2 %while.46 = (s32[]{:T(128)}, f32[4,128,512]{2,1,0:T(8,128)S(1)}, s32[]{:T(128)}, f32[128,512]{1,0:T(8,128)S(1)}, f32[128,512]{1,0:T(8,128)S(1)}, /*index=5*/f32[...) while((s32[]{:T(128)}, f32[4,128,512]{2,1,0:T(8,128)S(1)}, ...), condition=%wide.region_3.4_spmd, body=%wide.region_2.3_spmd.sunk | while | flops 2621443 | bytes 6553719 | solution.py:59
  72.4 28.1 %while.47 = (s32[]{:T(128)}, f32[4,128,512]{2,1,0:T(8,128)}, s32[]{:T(128)}, f32[128,512]{1,0:T(8,128)S(1)}, f32[128,512]{1,0:T(8,128)S(1)}, /*index=5*/f32[128,...) while((s32[]{:T(128)}, f32[4,128,512]{2,1,0:T(8,128)}, ...), condition=%wide.region_5.6_spmd, body=%wide.region_4.5_spmd.sunk | while | flops 2621443 | bytes 6553719 | solution.py:59
  73.0 1.2 copy.42
  74.3 1.6 fusion.48
  76.6 1.2 copy.42
  77.8 1.6 fusion.48
  80.1 1.2 copy.42
  81.3 1.6 fusion.48
  84.8 1.6 fusion.48
  87.1 1.2 copy.42
  88.3 1.6 fusion.48
  90.6 1.2 copy.42
  91.8 1.6 fusion.48
  95.3 1.6 fusion.48
  98.8 1.6 fusion.48
  100.5 1.9 %copy.11 = f32[4,128,512]{2,0,1:T(4,128)S(1)} copy(f32[4,128,512]{2,1,0:T(8,128)} %get-tuple-element.667) | data formatting | bytes 2097152 | tf_op jit(solution)/shard_map/while | solution.py:59
  102.4 59.1 %all_to_all.23 = f32[4,128,512]{2,0,1:T(4,128)S(1)} all-to-all(f32[4,128,512]{2,0,1:T(4,128)S(1)} %copy.11), channel_id=1, replica_groups=mesh['member'=4,'gx'=32] {'gx'}, dimensions={1} | all-to-all | bytes 2097152 | tf_op jit(solution)/shard_map/all_to_all | solution.py:73
  161.9 1.9 %convolution_bitcast_fusion = f32[128,4,512]{0,2,1:T(8,128)S(1)} fusion(f32[128,4,512]{2,1,0:T(4,128)S(1)} %bitcast.13, f32[128,128]{1,0:T(8,128)S(1)} %copy-done), kind=kOutput, calls=%fused_computation.42 | convolution fusion | flops 402653184 | bytes 2162688 | tf_op jit(solution)/shard_map/lk,kxy->lxy/dot_general | solution.py:74
  163.8 1.4 copy.14
  (52 shorter events, 23.9 us)
Async XLA Ops:
  0.0 161.9 %copy-start = (f32[128,128]{1,0:T(8,128)S(1)}, f32[128,128]{1,0:T(8,128)}, u32[]{:S(2)}) copy-start(f32[128,128]{1,0:T(8,128)} %param.12) | copy-start | bytes 196612
  1.5 40.6 %all-to-all-start = ((f32[32,4,512]{2,1,0:T(4,128)}), f32[32,4,512]{2,1,0:T(4,128)S(1)}, u32[]{:S(2)}, u32[]{:S(2)}) async-start(f32[32,4,512]{2,1,0:T(4,128)} %broadcast_in_dim.57), calls=%async_computation | async-start | bytes 524288 | tf_op jit(solution)/shard_map/all_to_all | solution.py:11
  20.0 1.2 copy-start.3
  42.2 0.7 copy-start.2
  43.0 2.0 %copy-start.1 = (f32[4,128,512]{2,1,0:T(8,128)S(1)}, f32[4,128,512]{2,1,0:T(8,128)}, u32[]{:S(2)}) copy-start(f32[4,128,512]{2,1,0:T(8,128)} %param.11) | copy-start | bytes 3145732
where the time goes:
time: 166 us; the launch traced here: 165 us
  blocking collectives  59.1 us (36%)
  other arithmetic  30.5 us (18%)
  waiting for transfers between devices  20.2 us (12%)
  local copies, waits for them, and re-layouts  19 us (11%)
  starting transfers between devices  18.5 us (11%)
  loops' own time  15.7 us (9%)
  matrix products  1.91 us (1%)
    all_to_all x1, blocking collectives, per_device(): lax.all_to_all(smooth, 'gx', split_axis=1, concat_axis=0, tiled=True)  59.1 us
    select_n x24, other arithmetic, sweep(): return jnp.where(index < count, updated, iterate)  27.8 us
    all_to_all x1, waiting for transfers between devices, sent_to_all(): lax.all_to_all(jnp.broadcast_to(array[None], (devices, *array.shape)), ax...  20.2 us
    all_to_all x1, starting transfers between devices, sent_to_all(): lax.all_to_all(jnp.broadcast_to(array[None], (devices, *array.shape)), ax...  18.5 us
    another operation x3, loops' own time, diffuse(): field = lax.fori_loop(0, SWEEP_MOST, sweep, source)  15.7 us
    while x24, local copies, waits for them, and re-layouts  10.9 us
  transfers between devices with their start and end apart: 1, of which 1 were waited for; matrix products, arithmetic and copies ran while one was open for 1% of the time, Pallas kernels for 0%

commit v1 on v0

v1 whole, which is shorter than its diff:
```python
import functools

import jax
import jax.numpy as jnp
from jax import lax
from jax.experimental import pallas as pl
from jax.experimental.pallas import tpu as pltpu
from jax.sharding import PartitionSpec as P

SWEEP_MOST = 8
SWEEP_LEAST = 4
LANES = 128
SUBS = 8
MESH = pl.DeviceIdType.MESH


def kernel(devices, levels, rows, pert, vert, kappa, mask, sweeps, out,
           xin, vin, kin, min_, cnt, kb, coef, u, src, sb, rb, lhs,
           load_sem, one_send, one_recv, two_send, two_recv, swap_send, swap_recv,
           send_sem, recv_sem):
    chips = devices // 2
    steps = rows // SUBS
    blocks = pert.shape[2] // LANES
    own = rows // devices
    slot = own * blocks
    me = lax.axis_index("gx")
    chip = me // 2
    core = lax.rem(me, 2)

    def at(dz, which):
        return lax.rem(chip + dz + chips, chips) * 2 + which

    partner = at(0, 1 - core)
    reach = chips // 4

    barrier = pltpu.get_barrier_semaphore()
    near = [at(s * d, core) for d in range(1, reach + 1) for s in (1, -1)] + [partner]
    for device in near:
        pl.semaphore_signal(barrier, inc=1, device_id={"gx": device}, device_id_type=MESH)

    loads = [
        pltpu.make_async_copy(kappa, kin, load_sem.at[0]),
        pltpu.make_async_copy(mask, min_, load_sem.at[1]),
        pltpu.make_async_copy(sweeps, cnt, load_sem.at[2]),
        pltpu.make_async_copy(vert, vin, load_sem.at[3]),
    ]
    for cb in range(blocks):
        loads.append(pltpu.make_async_copy(
            pert.at[:, :, pl.ds(cb * LANES, LANES)], xin.at[:, cb], load_sem.at[4 + cb]))
    for load in loads:
        load.start()
    loads[0].wait()
    loads[1].wait()
    for cb in range(blocks):
        lanes = pl.ds(cb * LANES, LANES)
        kb[me, pl.ds(cb * own, own), :] = kin[:, lanes] * min_[:, lanes].astype(jnp.float32)

    pl.semaphore_wait(barrier, len(near))

    def give(block, device, ssem, rsem):
        copy = pltpu.make_async_remote_copy(
            src_ref=kb.at[block], dst_ref=kb.at[block], send_sem=ssem, recv_sem=rsem,
            device_id={"gx": device}, device_id_type=MESH)
        copy.start()

    give(me, at(reach, core), one_send, one_recv.at[0])
    give(me, at(-reach, core), one_send, one_recv.at[1])
    for d in range(reach - 1, 0, -1):
        give(me, at(d, core), one_send, one_recv.at[2])
        give(me, at(-d, core), one_send, one_recv.at[2])

    for load in loads[2:]:
        load.wait()
    v = vin[...]
    vh = v.astype(jnp.bfloat16)
    vl = (v - vh.astype(jnp.float32)).astype(jnp.bfloat16)
    depth = lhs.shape[2]
    k_of = lax.broadcasted_iota(jnp.int32, (v.shape[1], depth), 0)
    j_of = lax.broadcasted_iota(jnp.int32, (v.shape[1], depth), 1)
    for c in range(levels):
        pick = k_of == lax.rem(j_of, devices) * levels + c
        high = jnp.where(pick & (j_of < 2 * devices), 1.0, 0.0).astype(jnp.bfloat16)
        low = jnp.where(pick & (j_of >= 2 * devices), 1.0, 0.0).astype(jnp.bfloat16)
        lhs[c] = (jnp.dot(vh, high, preferred_element_type=jnp.float32)
                  + jnp.dot(vl, low, preferred_element_type=jnp.float32)).astype(jnp.bfloat16)

    def arrived(blocks_, sem):
        pltpu.make_async_copy(kb.at[pl.ds(0, blocks_)], kb.at[pl.ds(0, blocks_)], sem).wait()

    arrived(1, one_recv.at[0])
    for d in range(reach, 0, -1):
        give(at(-reach, core), at(d, core), two_send, two_recv)
    arrived(1, one_recv.at[1])
    for d in range(reach - 1, 0, -1):
        give(at(reach, core), at(-d, core), two_send, two_recv)
    arrived(2 * reach - 2, one_recv.at[2])
    arrived(2 * reach - 1, two_recv)

    pairs = kb.reshape(chips, 2, slot, LANES)
    swap = pltpu.make_async_remote_copy(
        src_ref=pairs.at[:, core], dst_ref=pairs.at[:, core], send_sem=swap_send,
        recv_sem=swap_recv, device_id={"gx": partner}, device_id_type=MESH)
    swap.start()
    swap.wait()
    arrived(2 * reach, one_send)
    arrived(2 * reach - 1, two_send)

    kflat = kb.reshape(devices * slot, LANES)
    lane = lax.broadcasted_iota(jnp.int32, (SUBS, LANES), 1)
    sub = lax.broadcasted_iota(jnp.int32, (SUBS, LANES), 0)
    first = lane == 0
    last = lane == LANES - 1
    stride = steps // own * slot

    def place(t, cb):
        return pl.ds(t // own * slot + cb * own + t % own, SUBS, stride=stride)

    def west_of(row, cb, rolled, edge):
        return edge if cb == 0 else jnp.where(first, rolled[cb - 1], rolled[cb])

    def east_of(row, cb, rolled, edge):
        return edge if cb == blocks - 1 else jnp.where(last, rolled[cb + 1], rolled[cb])

    for t in range(steps):
        for cb in range(blocks):
            u[t, cb] = kflat[place(t, cb), :]
    for t in range(steps):
        cur = [u[t, cb] for cb in range(blocks)]
        if t > 0:
            up = [u[t - 1, cb] for cb in range(blocks)]
        else:
            up = [jnp.where(sub == 0, 0.0, pltpu.roll(u[steps - 1, cb], 1, 0)) for cb in range(blocks)]
        if t < steps - 1:
            down = [u[t + 1, cb] for cb in range(blocks)]
        else:
            down = [jnp.where(sub == SUBS - 1, 0.0, pltpu.roll(u[0, cb], SUBS - 1, 0)) for cb in range(blocks)]
        right = [pltpu.roll(c, 1, 1) for c in cur]
        left = [pltpu.roll(c, LANES - 1, 1) for c in cur]
        for cb in range(blocks):
            k = cur[cb]
            half = jnp.where(k > 0.0, 0.5, 0.0)
            sides = []
            for other in (up[cb], down[cb],
                          west_of(cur, cb, right, jnp.where(first, 0.0, right[0])),
                          east_of(cur, cb, left, jnp.where(last, 0.0, left[-1]))):
                sides.append(half * jnp.where(other > 0.0, k + other, 0.0))
            inv = 1.0 / (1.0 + sides[0] + sides[1] + sides[2] + sides[3])
            for i in range(4):
                coef[i, t, cb] = sides[i] * inv
            coef[4, t, cb] = inv

    def sweep(keep):
        top = [u[0, cb] for cb in range(blocks)]
        cur = top
        up = [pltpu.roll(u[steps - 1, cb], 1, 0) for cb in range(blocks)]
        for t in range(steps):
            if t < steps - 1:
                down = [u[t + 1, cb] for cb in range(blocks)]
            else:
                down = [pltpu.roll(c, SUBS - 1, 0) for c in top]
            right = [pltpu.roll(c, 1, 1) for c in cur]
            left = [pltpu.roll(c, LANES - 1, 1) for c in cur]
            for cb in range(blocks):
                new = (src[t, cb] + coef[0, t, cb] * up[cb] + coef[1, t, cb] * down[cb]
                       + (coef[2, t, cb] * west_of(cur, cb, right, right[0])
                          + coef[3, t, cb] * east_of(cur, cb, left, left[-1])))
                if keep is not None:
                    new = jnp.where(keep, new, cur[cb])
                u[t, cb] = new
            up, cur = cur, down

    order = []
    for d in range(chips // 2, 0, -1):
        for s in ((1,) if 2 * d == chips else (1, -1)):
            order += [at(s * d, 1 - core), at(s * d, core)]
    order.append(partner)

    @pl.loop(0, levels)
    def _(l):
        for t in range(steps):
            for cb in range(blocks):
                u[t, cb] = xin[l, cb, pl.ds(t, SUBS, stride=steps), :]

        @pl.loop(0, 3)
        def _(section):
            for t in range(steps):
                for cb in range(blocks):
                    src[t, cb] = u[t, cb] * coef[4, t, cb]
            count = jnp.full((SUBS, LANES), cnt[section], jnp.int32)

            @pl.loop(0, SWEEP_LEAST)
            def _(i):
                sweep(None)

            @pl.loop(SWEEP_LEAST, SWEEP_MOST)
            def _(i):
                sweep(count > i)

        for t in range(steps):
            for cb in range(blocks):
                sb[l, place(t, cb), :] = u[t, cb]
        here = pl.ds(pl.multiple_of(me * slot, slot), slot)
        for device in order:
            pltpu.make_async_remote_copy(
                src_ref=sb.at[l, pl.ds(pl.multiple_of(device * slot, slot), slot)],
                dst_ref=rb.at[l, here], send_sem=send_sem.at[l], recv_sem=recv_sem.at[l],
                device_id={"gx": device}, device_id_type=MESH).start()
        rb[l, here, :] = sb[l, here, :]

    others = pl.ds(0, (devices - 1) * slot)
    width = blocks * LANES

    @pl.loop(0, levels)
    def _(c):
        pltpu.make_async_copy(rb.at[c, others], rb.at[c, others], recv_sem.at[c]).wait()
        left = lhs[c]
        for r in range(own):
            tiles = []
            for cb in range(blocks):
                x = rb[c, pl.ds(cb * own + r, devices, stride=slot), :]
                xh = x.astype(jnp.bfloat16)
                xl = (x - xh.astype(jnp.float32)).astype(jnp.bfloat16)
                tiles.append(jnp.concatenate([xh, xl, xh], axis=0))
            part = jnp.dot(left, jnp.concatenate(tiles, axis=1), preferred_element_type=jnp.float32)
            columns = pl.ds(r * width, width)

            @pl.when(c == 0)
            def _():
                out[:, columns] = part

            @pl.when(c > 0)
            def _():
                out[:, columns] += part

    @pl.loop(0, levels)
    def _(l):
        pltpu.make_async_copy(sb.at[l, others], sb.at[l, others], send_sem.at[l]).wait()


def per_device(perturbation, vertical, kappa, sea_mask, sweeps):
    devices = lax.axis_size("gx")
    levels, rows, columns = perturbation.shape
    own = rows // devices
    blocks = columns // LANES
    steps = rows // SUBS
    slot = own * blocks
    total = vertical.shape[0]
    f32 = jnp.float32
    dma = pltpu.SemaphoreType.DMA
    result = pl.pallas_call(
        functools.partial(kernel, devices, levels, rows),
        out_shape=jax.ShapeDtypeStruct((total, own * columns), f32),
        in_specs=[pl.BlockSpec(memory_space=pl.ANY)] * 5,
        out_specs=pl.BlockSpec(memory_space=pltpu.VMEM),
        scratch_shapes=[
            pltpu.VMEM((levels, blocks, rows, LANES), f32),
            pltpu.VMEM(vertical.shape, f32),
            pltpu.VMEM(kappa.shape, f32),
            pltpu.VMEM(sea_mask.shape, jnp.int32),
            pltpu.SMEM(sweeps.shape, jnp.int32),
            pltpu.VMEM((devices, slot, LANES), f32),
            pltpu.VMEM((5, steps, blocks, SUBS, LANES), f32),
            pltpu.VMEM((steps, blocks, SUBS, LANES), f32),
            pltpu.VMEM((steps, blocks, SUBS, LANES), f32),
            pltpu.VMEM((levels, devices * slot, LANES), f32),
            pltpu.VMEM((levels, devices * slot, LANES), f32),
            pltpu.VMEM((levels, total, 3 * devices), jnp.bfloat16),
            dma((4 + blocks,)),
            dma(()), dma((3,)), dma(()), dma(()), dma(()), dma(()),
            dma((levels,)), dma((levels,)),
        ],
        compiler_params=pltpu.CompilerParams(collective_id=0, has_side_effects=True),
        name="smooth_and_send",
    )(perturbation, vertical, kappa, sea_mask, sweeps)
    return result.reshape(total, own, columns)


def solution(mesh):
    in_specs = (
        P(("member", "gx"), None, None),
        P("member", None),
        P(("member", "gx"), None),
        P("gx", None),
        P("member"),
    )
    out_specs = P("member", "gx", None)
    return jax.shard_map(
        per_device, mesh=mesh, in_specs=in_specs, out_specs=out_specs, check_vma=False
    )
```

time: 166 us -> 83.2 us (0.50)
  Pallas kernels: 0 us -> 80.1 us
  blocking collectives: 59.1 us -> 0 us
  other arithmetic: 30.5 us -> 0 us
  waiting for transfers between devices: 20.2 us -> 0 us
  starting transfers between devices: 18.5 us -> 0 us
  local copies, waits for them, and re-layouts: 19 us -> 2.9 us
  loops' own time: 15.7 us -> 0 us
  matrix products: 1.91 us -> 0 us
    pallas_call x0 -> x1, Pallas kernels: none -> 80.1 us  [per_device(): pl.pallas_call(functools.partial(kernel, devices, levels, rows), out_shap...]
    all_to_all x1 -> x0, blocking collectives: 59.1 us -> none  [per_device(): lax.all_to_all(smooth, 'gx', split_axis=1, concat_axis=0, tiled=True)]
    select_n x25 -> x0, other arithmetic: 27.8 us -> none  [the longest x24 27.8 us: sweep(): return jnp.where(index < count, updated, iterate)]
    all_to_all x1 -> x0, waiting for transfers between devices: 20.2 us -> none  [sent_to_all(): lax.all_to_all(jnp.broadcast_to(array[None], (devices, *array.shape)), ax...]
    all_to_all x1 -> x0, starting transfers between devices: 18.5 us -> none  [sent_to_all(): lax.all_to_all(jnp.broadcast_to(array[None], (devices, *array.shape)), ax...]
    another operation x3 -> x0, loops' own time: 15.7 us -> none  [diffuse(): field = lax.fori_loop(0, SWEEP_MOST, sweep, source)]
    while x25 -> x0, local copies, waits for them, and re-layouts: 12.8 us -> none
    unnamed x11 -> x0, local copies, waits for them, and re-layouts: 2.94 us -> none
  transfers between devices with their start and end apart: 1 -> 0, of which waited for: 1 -> 0; matrix products, arithmetic and copies ran while one was open for 1% -> 0% of each run, Pallas kernels for 0% -> 0%
where the time goes in v1:
time: 83.2 us; the launch traced here: 83 us
  Pallas kernels  80.1 us (96%)
  local copies, waits for them, and re-layouts  2.9 us (3%)
    pallas_call x1, Pallas kernels, per_device(): pl.pallas_call(functools.partial(kernel, devices, levels, rows), out_shap...  80.1 us
    reshape x1, local copies, waits for them, and re-layouts, per_device(): return result.reshape(total, own, columns)  2.9 us

profile of v1, /device:TPU:69, one launch (start us, length us, event | category | flops | bytes accessed | tf_op | source)
XLA Modules:
  0.0 83.0 jit_solution(11586640331377604479)
XLA Ops:
  0.0 80.1 %smooth_and_send.1 = f32[128,2048]{1,0:T(8,128)} custom-call(f32[4,128,512]{2,1,0:T(8,128)} %pert.1, f32[128,128]{1,0:T(8,128)} %vert.1, f32[4,512]{1,0:T(4,128)} %kappa.1, s32[4,512]{1,0:T(4,128)} %mask.1, s32[3]{0:T(128)} %sweeps.1), custom_call_target="tpu_custom_call" | custom-call | tf_op jit(solution)/shard_map/smooth_and_send/pallas_call | solution.py:250
  80.1 2.9 %reshape.3 = f32[128,4,512]{2,1,0:T(4,128)} reshape(f32[128,2048]{1,0:T(8,128)} %smooth_and_send.1) | data formatting | bytes 2097152 | tf_op jit(solution)/shard_map/reshape | solution.py:275

commit v2 on v1

--- a/solution.py
+++ b/solution.py
@@ -15,9 +15,8 @@
 
 
 def kernel(devices, levels, rows, pert, vert, kappa, mask, sweeps, out,
-           xin, vin, kin, min_, cnt, kb, coef, u, src, sb, rb, lhs,
-           load_sem, one_send, one_recv, two_send, two_recv, swap_send, swap_recv,
-           send_sem, recv_sem):
+           xin, vin, kin, min_, cnt, kb, coef, xi, src, sb, rb, lhs,
+           load_sem, one_send, one_recv, two_send, two_recv, send_sem, recv_sem):
     chips = devices // 2
     steps = rows // SUBS
     blocks = pert.shape[2] // LANES
@@ -33,8 +32,34 @@
     partner = at(0, 1 - core)
     reach = chips // 4
 
+    lane = lax.broadcasted_iota(jnp.int32, (SUBS, LANES), 1)
+    sub = lax.broadcasted_iota(jnp.int32, (SUBS, LANES), 0)
+    group = LANES // blocks
+    low64 = lane < LANES // 2
+    low32 = lax.rem(lane, LANES // 2) < group
+
+    def transposed(v):
+        a = [None] * 4
+        for i in (0, 1):
+            a[i] = jnp.where(low64, v[i], pltpu.roll(v[i + 2], LANES // 2, 1))
+            a[i + 2] = jnp.where(low64, pltpu.roll(v[i], LANES // 2, 1), v[i + 2])
+        b = [None] * 4
+        for i in (0, 2):
+            b[i] = jnp.where(low32, a[i], pltpu.roll(a[i + 1], group, 1))
+            b[i + 1] = jnp.where(low32, pltpu.roll(a[i], LANES - group, 1), a[i + 1])
+        return b
+
+    def picked(v, index):
+        return [jnp.take_along_axis(x, index, axis=1, mode="promise_in_bounds") for x in v]
+
+    def interleaved(v):
+        return transposed(picked(v, lax.rem(lane, group) * blocks + lane // group))
+
+    def natural(v):
+        return picked(transposed(v), lax.rem(lane, blocks) * group + lane // blocks)
+
     barrier = pltpu.get_barrier_semaphore()
-    near = [at(s * d, core) for d in range(1, reach + 1) for s in (1, -1)] + [partner]
+    near = [at(s * d, c) for d in range(1, reach + 1) for s in (1, -1) for c in (core, 1 - core)] + [partner]
     for device in near:
         pl.semaphore_signal(barrier, inc=1, device_id={"gx": device}, device_id_type=MESH)
 
@@ -51,9 +76,13 @@
         load.start()
     loads[0].wait()
     loads[1].wait()
+    wet = []
     for cb in range(blocks):
         lanes = pl.ds(cb * LANES, LANES)
-        kb[me, pl.ds(cb * own, own), :] = kin[:, lanes] * min_[:, lanes].astype(jnp.float32)
+        x = kin[:, lanes] * min_[:, lanes].astype(jnp.float32)
+        wet.append(jnp.concatenate([x, jnp.zeros((SUBS - own, LANES), jnp.float32)], axis=0))
+    for cb, x in enumerate(interleaved(wet)):
+        kb[me, pl.ds(cb * own, own), :] = x[:own]
 
     pl.semaphore_wait(barrier, len(near))
 
@@ -65,9 +94,13 @@
 
     give(me, at(reach, core), one_send, one_recv.at[0])
     give(me, at(-reach, core), one_send, one_recv.at[1])
+    give(me, at(reach, 1 - core), one_send, one_recv.at[2])
+    give(me, at(-reach, 1 - core), one_send, one_recv.at[2])
     for d in range(reach - 1, 0, -1):
-        give(me, at(d, core), one_send, one_recv.at[2])
-        give(me, at(-d, core), one_send, one_recv.at[2])
+        for c in (core, 1 - core):
+            give(me, at(d, c), one_send, one_recv.at[2])
+            give(me, at(-d, c), one_send, one_recv.at[2])
+    give(me, partner, one_send, one_recv.at[2])
 
     for load in loads[2:]:
         load.wait()
@@ -89,25 +122,26 @@
 
     arrived(1, one_recv.at[0])
     for d in range(reach, 0, -1):
-        give(at(-reach, core), at(d, core), two_send, two_recv)
+        for c in (core, 1 - core):
+            give(at(-reach, core), at(d, c), two_send, two_recv)
     arrived(1, one_recv.at[1])
     for d in range(reach - 1, 0, -1):
-        give(at(reach, core), at(-d, core), two_send, two_recv)
-    arrived(2 * reach - 2, one_recv.at[2])
-    arrived(2 * reach - 1, two_recv)
-
-    pairs = kb.reshape(chips, 2, slot, LANES)
-    swap = pltpu.make_async_remote_copy(
-        src_ref=pairs.at[:, core], dst_ref=pairs.at[:, core], send_sem=swap_send,
-        recv_sem=swap_recv, device_id={"gx": partner}, device_id_type=MESH)
-    swap.start()
-    swap.wait()
-    arrived(2 * reach, one_send)
-    arrived(2 * reach - 1, two_send)
+        for c in (core, 1 - core):
+            give(at(reach, core), at(-d, c), two_send, two_recv)
+
+    @pl.loop(0, levels)
+    def _(l):
+        for t in range(steps):
+            v = [xin[l, cb, pl.ds(t, SUBS, stride=steps), :] for cb in range(blocks)]
+            for cb, x in enumerate(interleaved(v)):
+                xi[l, t, cb] = x
+
+    arrived(4 * reach - 1, one_recv.at[2])
+    arrived(4 * reach - 2, two_recv)
+    arrived(4 * reach + 1, one_send)
+    arrived(4 * reach - 2, two_send)
 
     kflat = kb.reshape(devices * slot, LANES)
-    lane = lax.broadcasted_iota(jnp.int32, (SUBS, LANES), 1)
-    sub = lax.broadcasted_iota(jnp.int32, (SUBS, LANES), 0)
     first = lane == 0
     last = lane == LANES - 1
     stride = steps // own * slot
@@ -115,41 +149,34 @@
     def place(t, cb):
         return pl.ds(t // own * slot + cb * own + t % own, SUBS, stride=stride)
 
-    def west_of(row, cb, rolled, edge):
-        return edge if cb == 0 else jnp.where(first, rolled[cb - 1], rolled[cb])
-
-    def east_of(row, cb, rolled, edge):
-        return edge if cb == blocks - 1 else jnp.where(last, rolled[cb + 1], rolled[cb])
-
+    ks = src
     for t in range(steps):
         for cb in range(blocks):
-            u[t, cb] = kflat[place(t, cb), :]
+            ks[t, cb] = kflat[place(t, cb), :]
     for t in range(steps):
-        cur = [u[t, cb] for cb in range(blocks)]
+        cur = [ks[t, cb] for cb in range(blocks)]
         if t > 0:
-            up = [u[t - 1, cb] for cb in range(blocks)]
+            up = [ks[t - 1, cb] for cb in range(blocks)]
         else:
-            up = [jnp.where(sub == 0, 0.0, pltpu.roll(u[steps - 1, cb], 1, 0)) for cb in range(blocks)]
+            up = [jnp.where(sub == 0, 0.0, pltpu.roll(ks[steps - 1, cb], 1, 0)) for cb in range(blocks)]
         if t < steps - 1:
-            down = [u[t + 1, cb] for cb in range(blocks)]
+            down = [ks[t + 1, cb] for cb in range(blocks)]
         else:
-            down = [jnp.where(sub == SUBS - 1, 0.0, pltpu.roll(u[0, cb], SUBS - 1, 0)) for cb in range(blocks)]
-        right = [pltpu.roll(c, 1, 1) for c in cur]
-        left = [pltpu.roll(c, LANES - 1, 1) for c in cur]
+            down = [jnp.where(sub == SUBS - 1, 0.0, pltpu.roll(ks[0, cb], SUBS - 1, 0)) for cb in range(blocks)]
+        west = [jnp.where(first, 0.0, pltpu.roll(cur[-1], 1, 1))] + cur[:-1]
+        east = cur[1:] + [jnp.where(last, 0.0, pltpu.roll(cur[0], LANES - 1, 1))]
         for cb in range(blocks):
             k = cur[cb]
             half = jnp.where(k > 0.0, 0.5, 0.0)
             sides = []
-            for other in (up[cb], down[cb],
-                          west_of(cur, cb, right, jnp.where(first, 0.0, right[0])),
-                          east_of(cur, cb, left, jnp.where(last, 0.0, left[-1]))):
+            for other in (up[cb], down[cb], west[cb], east[cb]):
                 sides.append(half * jnp.where(other > 0.0, k + other, 0.0))
             inv = 1.0 / (1.0 + sides[0] + sides[1] + sides[2] + sides[3])
             for i in range(4):
                 coef[i, t, cb] = sides[i] * inv
             coef[4, t, cb] = inv
 
-    def sweep(keep):
+    def sweep(u, keep):
         top = [u[0, cb] for cb in range(blocks)]
         cur = top
         up = [pltpu.roll(u[steps - 1, cb], 1, 0) for cb in range(blocks)]
@@ -158,12 +185,11 @@
                 down = [u[t + 1, cb] for cb in range(blocks)]
             else:
                 down = [pltpu.roll(c, SUBS - 1, 0) for c in top]
-            right = [pltpu.roll(c, 1, 1) for c in cur]
-            left = [pltpu.roll(c, LANES - 1, 1) for c in cur]
+            west = [pltpu.roll(cur[-1], 1, 1)] + cur[:-1]
+            east = cur[1:] + [pltpu.roll(cur[0], LANES - 1, 1)]
             for cb in range(blocks):
                 new = (src[t, cb] + coef[0, t, cb] * up[cb] + coef[1, t, cb] * down[cb]
-                       + (coef[2, t, cb] * west_of(cur, cb, right, right[0])
-                          + coef[3, t, cb] * east_of(cur, cb, left, left[-1])))
+                       + (coef[2, t, cb] * west[cb] + coef[3, t, cb] * east[cb]))
                 if keep is not None:
                     new = jnp.where(keep, new, cur[cb])
                 u[t, cb] = new
@@ -177,9 +203,7 @@
 
     @pl.loop(0, levels)
     def _(l):
-        for t in range(steps):
-            for cb in range(blocks):
-                u[t, cb] = xin[l, cb, pl.ds(t, SUBS, stride=steps), :]
+        u = xi.at[l]
 
         @pl.loop(0, 3)
         def _(section):
@@ -190,15 +214,15 @@
 
             @pl.loop(0, SWEEP_LEAST)
             def _(i):
-                sweep(None)
+                sweep(u, None)
 
             @pl.loop(SWEEP_LEAST, SWEEP_MOST)
             def _(i):
-                sweep(count > i)
+                sweep(u, count > i)
 
         for t in range(steps):
-            for cb in range(blocks):
-                sb[l, place(t, cb), :] = u[t, cb]
+            for cb, x in enumerate(natural([u[t, cb] for cb in range(blocks)])):
+                sb[l, place(t, cb), :] = x
         here = pl.ds(pl.multiple_of(me * slot, slot), slot)
         for device in order:
             pltpu.make_async_remote_copy(
@@ -260,13 +284,13 @@
             pltpu.SMEM(sweeps.shape, jnp.int32),
             pltpu.VMEM((devices, slot, LANES), f32),
             pltpu.VMEM((5, steps, blocks, SUBS, LANES), f32),
-            pltpu.VMEM((steps, blocks, SUBS, LANES), f32),
+            pltpu.VMEM((levels, steps, blocks, SUBS, LANES), f32),
             pltpu.VMEM((steps, blocks, SUBS, LANES), f32),
             pltpu.VMEM((levels, devices * slot, LANES), f32),
             pltpu.VMEM((levels, devices * slot, LANES), f32),
             pltpu.VMEM((levels, total, 3 * devices), jnp.bfloat16),
             dma((4 + blocks,)),
-            dma(()), dma((3,)), dma(()), dma(()), dma(()), dma(()),
+            dma(()), dma((3,)), dma(()), dma(()),
             dma((levels,)), dma((levels,)),
         ],
         compiler_params=pltpu.CompilerParams(collective_id=0, has_side_effects=True),

time: 83.2 us -> 81.5 us (0.980)
  Pallas kernels: 80.1 us -> 78.5 us
    pallas_call x1, Pallas kernels: 80.1 us -> 78.5 us  [per_device(): pl.pallas_call(functools.partial(kernel, devices, levels, rows), out_shap...]
where the time goes in v2:
time: 81.5 us; the launch traced here: 81.4 us
  Pallas kernels  78.5 us (96%)
  local copies, waits for them, and re-layouts  2.9 us (4%)
    pallas_call x1, Pallas kernels, per_device(): pl.pallas_call(functools.partial(kernel, devices, levels, rows), out_shap...  78.5 us
    reshape x1, local copies, waits for them, and re-layouts, per_device(): return result.reshape(total, own, columns)  2.9 us

profile of v2, /device:TPU:69, one launch (start us, length us, event | category | flops | bytes accessed | tf_op | source)
XLA Modules:
  0.0 81.4 jit_solution(7946061584839602259)
XLA Ops:
  0.0 78.5 %smooth_and_send.1 = f32[128,2048]{1,0:T(8,128)} custom-call(f32[4,128,512]{2,1,0:T(8,128)} %pert.1, f32[128,128]{1,0:T(8,128)} %vert.1, f32[4,512]{1,0:T(4,128)} %kappa.1, s32[4,512]{1,0:T(4,128)} %mask.1, s32[3]{0:T(128)} %sweeps.1), custom_call_target="tpu_custom_call" | custom-call | tf_op jit(solution)/shard_map/smooth_and_send/pallas_call | solution.py:274
  78.5 2.9 %reshape.3 = f32[128,4,512]{2,1,0:T(4,128)} reshape(f32[128,2048]{1,0:T(8,128)} %smooth_and_send.1) | data formatting | bytes 2097152 | tf_op jit(solution)/shard_map/reshape | solution.py:299

commit v3 on v2

--- a/solution.py
+++ b/solution.py
@@ -27,7 +27,7 @@
     core = lax.rem(me, 2)
 
     def at(dz, which):
-        return lax.rem(chip + dz + chips, chips) * 2 + which
+        return lax.rem(me + 2 * (dz + chips), devices) - core + which
 
     partner = at(0, 1 - core)
     reach = chips // 4
@@ -59,10 +59,6 @@
         return picked(transposed(v), lax.rem(lane, blocks) * group + lane // blocks)
 
     barrier = pltpu.get_barrier_semaphore()
-    near = [at(s * d, c) for d in range(1, reach + 1) for s in (1, -1) for c in (core, 1 - core)] + [partner]
-    for device in near:
-        pl.semaphore_signal(barrier, inc=1, device_id={"gx": device}, device_id_type=MESH)
-
     loads = [
         pltpu.make_async_copy(kappa, kin, load_sem.at[0]),
         pltpu.make_async_copy(mask, min_, load_sem.at[1]),
@@ -72,7 +68,13 @@
     for cb in range(blocks):
         loads.append(pltpu.make_async_copy(
             pert.at[:, :, pl.ds(cb * LANES, LANES)], xin.at[:, cb], load_sem.at[4 + cb]))
-    for load in loads:
+    for load in loads[:2]:
+        load.start()
+    near = [at(s * d, c) for d in range(1, reach + 1) for s in (1, -1) for c in (core, 1 - core)] + [partner]
+    for device in near:
+        pl.semaphore_signal(barrier, inc=1, device_id={"gx": device}, device_id_type=MESH)
+
+    for load in loads[2:]:
         load.start()
     loads[0].wait()
     loads[1].wait()
@@ -195,11 +197,16 @@
                 u[t, cb] = new
             up, cur = cur, down
 
-    order = []
-    for d in range(chips // 2, 0, -1):
-        for s in ((1,) if 2 * d == chips else (1, -1)):
-            order += [at(s * d, 1 - core), at(s * d, core)]
-    order.append(partner)
+    here = pl.ds(pl.multiple_of(me * slot, slot), slot)
+    early = devices // 4
+
+    def post(l, wanted):
+        for j in wanted:
+            device = jnp.where(me == j, devices - 1, j)
+            pltpu.make_async_remote_copy(
+                src_ref=sb.at[l, pl.ds(pl.multiple_of(device * slot, slot), slot)],
+                dst_ref=rb.at[l, here], send_sem=send_sem.at[l], recv_sem=recv_sem.at[l],
+                device_id={"gx": device}, device_id_type=MESH).start()
 
     @pl.loop(0, levels)
     def _(l):
@@ -223,13 +230,17 @@
         for t in range(steps):
             for cb, x in enumerate(natural([u[t, cb] for cb in range(blocks)])):
                 sb[l, place(t, cb), :] = x
-        here = pl.ds(pl.multiple_of(me * slot, slot), slot)
-        for device in order:
-            pltpu.make_async_remote_copy(
-                src_ref=sb.at[l, pl.ds(pl.multiple_of(device * slot, slot), slot)],
-                dst_ref=rb.at[l, here], send_sem=send_sem.at[l], recv_sem=recv_sem.at[l],
-                device_id={"gx": device}, device_id_type=MESH).start()
+        post(l, range(early))
+
+        @pl.when(l == 0)
+        def _():
+            post(l, range(early, devices - 1))
+
         rb[l, here, :] = sb[l, here, :]
+
+    @pl.loop(1, levels)
+    def _(l):
+        post(l, range(early, devices - 1))
 
     others = pl.ds(0, (devices - 1) * slot)
     width = blocks * LANES
@@ -273,7 +284,7 @@
     dma = pltpu.SemaphoreType.DMA
     result = pl.pallas_call(
         functools.partial(kernel, devices, levels, rows),
-        out_shape=jax.ShapeDtypeStruct((total, own * columns), f32),
+        out_shape=pltpu.VMEM((total, own * columns), f32),
         in_specs=[pl.BlockSpec(memory_space=pl.ANY)] * 5,
         out_specs=pl.BlockSpec(memory_space=pltpu.VMEM),
         scratch_shapes=[

time: 81.5 us -> 74.9 us (0.919)
  the two profiles are of different devices: /device:TPU:69 before, /device:TPU:583 now
where the time goes in v3:
time: 74.9 us; the launch traced here: 74.7 us
  Pallas kernels  73.1 us (98%)
  local copies, waits for them, and re-layouts  1.68 us (2%)
    pallas_call x1, Pallas kernels, per_device(): pl.pallas_call(functools.partial(kernel, devices, levels, rows), out_shap...  73.1 us
    reshape x1, local copies, waits for them, and re-layouts, per_device(): return result.reshape(total, own, columns)  1.68 us

profile of v3, /device:TPU:583, one launch (start us, length us, event | category | flops | bytes accessed | tf_op | source)
XLA Modules:
  0.0 74.7 jit_solution(11183531179705823413)
XLA Ops:
  0.0 73.1 %smooth_and_send.1 = f32[128,2048]{1,0:T(8,128)S(1)} custom-call(f32[4,128,512]{2,1,0:T(8,128)} %pert.1, f32[128,128]{1,0:T(8,128)} %vert.1, f32[4,512]{1,0:T(4,128)} %kappa.1, s32[4,512]{1,0:T(4,128)} %mask.1, s32[3]{0:T(128)} %sweeps.1), custom_call_target="tpu_custom_call" | custom-call | tf_op jit(solution)/shard_map/smooth_and_send/pallas_call | solution.py:285
  73.1 1.7 %reshape.3 = f32[128,4,512]{2,1,0:T(4,128)} reshape(f32[128,2048]{1,0:T(8,128)S(1)} %smooth_and_send.1) | data formatting | bytes 2097152 | tf_op jit(solution)/shard_map/reshape | solution.py:310

commit v4 on v3

--- a/solution.py
+++ b/solution.py
@@ -15,8 +15,8 @@
 
 
 def kernel(devices, levels, rows, pert, vert, kappa, mask, sweeps, out,
-           xin, vin, kin, min_, cnt, kb, coef, xi, src, sb, rb, lhs,
-           load_sem, one_send, one_recv, two_send, two_recv, send_sem, recv_sem):
+           xin, vin, kin, min_, cnt, kb, coef, xi, src, sb, rb, lhs, acc,
+           load_sem, one_send, two_send, block_recv, send_sem, recv_sem):
     chips = devices // 2
     steps = rows // SUBS
     blocks = pert.shape[2] // LANES
@@ -88,21 +88,17 @@
 
     pl.semaphore_wait(barrier, len(near))
 
-    def give(block, device, ssem, rsem):
-        copy = pltpu.make_async_remote_copy(
-            src_ref=kb.at[block], dst_ref=kb.at[block], send_sem=ssem, recv_sem=rsem,
-            device_id={"gx": device}, device_id_type=MESH)
-        copy.start()
-
-    give(me, at(reach, core), one_send, one_recv.at[0])
-    give(me, at(-reach, core), one_send, one_recv.at[1])
-    give(me, at(reach, 1 - core), one_send, one_recv.at[2])
-    give(me, at(-reach, 1 - core), one_send, one_recv.at[2])
-    for d in range(reach - 1, 0, -1):
+    def give(block, device, ssem):
+        pltpu.make_async_remote_copy(
+            src_ref=kb.at[block], dst_ref=kb.at[block], send_sem=ssem,
+            recv_sem=block_recv.at[block],
+            device_id={"gx": device}, device_id_type=MESH).start()
+
+    for d in range(reach, 0, -1):
         for c in (core, 1 - core):
-            give(me, at(d, c), one_send, one_recv.at[2])
-            give(me, at(-d, c), one_send, one_recv.at[2])
-    give(me, partner, one_send, one_recv.at[2])
+            give(me, at(d, c), one_send)
+            give(me, at(-d, c), one_send)
+    give(me, partner, one_send)
 
     for load in loads[2:]:
         load.wait()
@@ -119,17 +115,28 @@
         lhs[c] = (jnp.dot(vh, high, preferred_element_type=jnp.float32)
                   + jnp.dot(vl, low, preferred_element_type=jnp.float32)).astype(jnp.bfloat16)
 
-    def arrived(blocks_, sem):
+    def sent(blocks_, sem):
         pltpu.make_async_copy(kb.at[pl.ds(0, blocks_)], kb.at[pl.ds(0, blocks_)], sem).wait()
 
-    arrived(1, one_recv.at[0])
+    def arrived(block):
+        pltpu.make_async_copy(kb.at[block], kb.at[block], block_recv.at[block]).wait()
+
+    below, above = at(-reach, core), at(reach, core)
+    arrived(below)
     for d in range(reach, 0, -1):
         for c in (core, 1 - core):
-            give(at(-reach, core), at(d, c), two_send, two_recv)
-    arrived(1, one_recv.at[1])
+            give(below, at(d, c), two_send)
+    arrived(above)
     for d in range(reach - 1, 0, -1):
         for c in (core, 1 - core):
-            give(at(reach, core), at(-d, c), two_send, two_recv)
+            give(above, at(-d, c), two_send)
+
+    def others_arrived(start, stop):
+        @pl.loop(start, stop)
+        def _(j):
+            @pl.when((j != me) & (j != below) & (j != above))
+            def _():
+                arrived(j)
 
     @pl.loop(0, levels)
     def _(l):
@@ -138,98 +145,104 @@
             for cb, x in enumerate(interleaved(v)):
                 xi[l, t, cb] = x
 
-    arrived(4 * reach - 1, one_recv.at[2])
-    arrived(4 * reach - 2, two_recv)
-    arrived(4 * reach + 1, one_send)
-    arrived(4 * reach - 2, two_send)
-
     kflat = kb.reshape(devices * slot, LANES)
     first = lane == 0
     last = lane == LANES - 1
-    stride = steps // own * slot
-
-    def place(t, cb):
-        return pl.ds(t // own * slot + cb * own + t % own, SUBS, stride=stride)
-
-    ks = src
-    for t in range(steps):
-        for cb in range(blocks):
-            ks[t, cb] = kflat[place(t, cb), :]
-    for t in range(steps):
-        cur = [ks[t, cb] for cb in range(blocks)]
-        if t > 0:
-            up = [ks[t - 1, cb] for cb in range(blocks)]
-        else:
-            up = [jnp.where(sub == 0, 0.0, pltpu.roll(ks[steps - 1, cb], 1, 0)) for cb in range(blocks)]
-        if t < steps - 1:
-            down = [ks[t + 1, cb] for cb in range(blocks)]
-        else:
-            down = [jnp.where(sub == SUBS - 1, 0.0, pltpu.roll(ks[0, cb], SUBS - 1, 0)) for cb in range(blocks)]
-        west = [jnp.where(first, 0.0, pltpu.roll(cur[-1], 1, 1))] + cur[:-1]
-        east = cur[1:] + [jnp.where(last, 0.0, pltpu.roll(cur[0], LANES - 1, 1))]
-        for cb in range(blocks):
-            k = cur[cb]
-            half = jnp.where(k > 0.0, 0.5, 0.0)
-            sides = []
-            for other in (up[cb], down[cb], west[cb], east[cb]):
-                sides.append(half * jnp.where(other > 0.0, k + other, 0.0))
-            inv = 1.0 / (1.0 + sides[0] + sides[1] + sides[2] + sides[3])
-            for i in range(4):
-                coef[i, t, cb] = sides[i] * inv
-            coef[4, t, cb] = inv
-
-    def sweep(u, keep):
-        top = [u[0, cb] for cb in range(blocks)]
-        cur = top
-        up = [pltpu.roll(u[steps - 1, cb], 1, 0) for cb in range(blocks)]
-        for t in range(steps):
-            if t < steps - 1:
-                down = [u[t + 1, cb] for cb in range(blocks)]
+
+    def place(t, cb, count):
+        return pl.ds(t // own * slot + cb * own + t % own, SUBS, stride=count // own * slot)
+
+    def couple(count):
+        ks = src
+        for t in range(count):
+            for cb in range(blocks):
+                ks[t, cb] = kflat[place(t, cb, count), :]
+        for t in range(count):
+            cur = [ks[t, cb] for cb in range(blocks)]
+            if t > 0:
+                up = [ks[t - 1, cb] for cb in range(blocks)]
             else:
-                down = [pltpu.roll(c, SUBS - 1, 0) for c in top]
+                up = [jnp.where(sub == 0, 0.0, pltpu.roll(ks[count - 1, cb], 1, 0)) for cb in range(blocks)]
+            if t < count - 1:
+                down = [ks[t + 1, cb] for cb in range(blocks)]
+            else:
+                down = [jnp.where(sub == SUBS - 1, 0.0, pltpu.roll(ks[0, cb], SUBS - 1, 0)) for cb in range(blocks)]
+            west = [jnp.where(first, 0.0, pltpu.roll(cur[-1], 1, 1))] + cur[:-1]
+            east = cur[1:] + [jnp.where(last, 0.0, pltpu.roll(cur[0], LANES - 1, 1))]
+            for cb in range(blocks):
+                k = cur[cb]
+                half = jnp.where(k > 0.0, 0.5, 0.0)
+                sides = []
+                for other in (up[cb], down[cb], west[cb], east[cb]):
+                    sides.append(half * jnp.where(other > 0.0, k + other, 0.0))
+                inv = 1.0 / (1.0 + sides[0] + sides[1] + sides[2] + sides[3])
+                for i in range(4):
+                    coef[i, t, cb] = sides[i] * inv
+                coef[4, t, cb] = inv
+
+    def sweep(u, count, start, keep):
+        def row(t):
+            return [u[t % count, cb] for cb in range(blocks)]
+
+        top = row(start)
+        up, cur = row(start - 1), top
+        for i in range(count):
+            t = (start + i) % count
+            down = row(t + 1) if i < count - 1 else top
+            north = [pltpu.roll(c, 1, 0) for c in up] if t == 0 else up
+            south = [pltpu.roll(c, SUBS - 1, 0) for c in down] if t == count - 1 else down
             west = [pltpu.roll(cur[-1], 1, 1)] + cur[:-1]
             east = cur[1:] + [pltpu.roll(cur[0], LANES - 1, 1)]
             for cb in range(blocks):
-                new = (src[t, cb] + coef[0, t, cb] * up[cb] + coef[1, t, cb] * down[cb]
+                new = (src[t, cb] + coef[0, t, cb] * north[cb] + coef[1, t, cb] * south[cb]
                        + (coef[2, t, cb] * west[cb] + coef[3, t, cb] * east[cb]))
                 if keep is not None:
                     new = jnp.where(keep, new, cur[cb])
                 u[t, cb] = new
             up, cur = cur, down
 
+    def diffuse(u, count, to):
+        @pl.loop(0, 3)
+        def _(section):
+            for t in range(count):
+                for cb in range(blocks):
+                    src[t, cb] = u[t, cb] * coef[4, t, cb]
+            most = jnp.full((SUBS, LANES), cnt[section], jnp.int32)
+
+            @pl.loop(0, SWEEP_LEAST, step=2)
+            def _(i):
+                sweep(u, count, 0, None)
+                sweep(u, count, 2, None)
+
+            @pl.loop(SWEEP_LEAST, SWEEP_MOST, step=2)
+            def _(i):
+                sweep(u, count, 0, most > i)
+                sweep(u, count, 2, most > i + 1)
+
+        for t in range(count):
+            for cb, x in enumerate(natural([u[t, cb] for cb in range(blocks)])):
+                to[place(t, cb, count), :] = x
+
     here = pl.ds(pl.multiple_of(me * slot, slot), slot)
     early = devices // 4
 
+    def send(l, rows_, device):
+        pltpu.make_async_remote_copy(
+            src_ref=rows_.at[pl.ds(pl.multiple_of(device * slot, slot), slot)],
+            dst_ref=rb.at[l, here], send_sem=send_sem.at[l], recv_sem=recv_sem.at[l],
+            device_id={"gx": device}, device_id_type=MESH).start()
+
     def post(l, wanted):
         for j in wanted:
-            device = jnp.where(me == j, devices - 1, j)
-            pltpu.make_async_remote_copy(
-                src_ref=sb.at[l, pl.ds(pl.multiple_of(device * slot, slot), slot)],
-                dst_ref=rb.at[l, here], send_sem=send_sem.at[l], recv_sem=recv_sem.at[l],
-                device_id={"gx": device}, device_id_type=MESH).start()
+            send(l, sb.at[l], jnp.where(me == j, devices - 1, j))
+
+    others_arrived(0, devices)
+    couple(steps)
 
     @pl.loop(0, levels)
     def _(l):
-        u = xi.at[l]
-
-        @pl.loop(0, 3)
-        def _(section):
-            for t in range(steps):
-                for cb in range(blocks):
-                    src[t, cb] = u[t, cb] * coef[4, t, cb]
-            count = jnp.full((SUBS, LANES), cnt[section], jnp.int32)
-
-            @pl.loop(0, SWEEP_LEAST)
-            def _(i):
-                sweep(u, None)
-
-            @pl.loop(SWEEP_LEAST, SWEEP_MOST)
-            def _(i):
-                sweep(u, count > i)
-
-        for t in range(steps):
-            for cb, x in enumerate(natural([u[t, cb] for cb in range(blocks)])):
-                sb[l, place(t, cb), :] = x
+        diffuse(xi.at[l], steps, sb.at[l])
+
         post(l, range(early))
 
         @pl.when(l == 0)
@@ -261,15 +274,22 @@
 
             @pl.when(c == 0)
             def _():
-                out[:, columns] = part
-
-            @pl.when(c > 0)
+                acc[:, columns] = part
+
+            @pl.when((c > 0) & (c < levels - 1))
             def _():
-                out[:, columns] += part
+                acc[:, columns] += part
+
+            @pl.when(c == levels - 1)
+            def _():
+                out[:, r, :] = acc[:, columns] + part
 
     @pl.loop(0, levels)
     def _(l):
         pltpu.make_async_copy(sb.at[l, others], sb.at[l, others], send_sem.at[l]).wait()
+
+    sent(4 * reach + 1, one_send)
+    sent(4 * reach - 2, two_send)
 
 
 def per_device(perturbation, vertical, kappa, sea_mask, sweeps):
@@ -284,7 +304,7 @@
     dma = pltpu.SemaphoreType.DMA
     result = pl.pallas_call(
         functools.partial(kernel, devices, levels, rows),
-        out_shape=pltpu.VMEM((total, own * columns), f32),
+        out_shape=pltpu.VMEM((total, own, columns), f32),
         in_specs=[pl.BlockSpec(memory_space=pl.ANY)] * 5,
         out_specs=pl.BlockSpec(memory_space=pltpu.VMEM),
         scratch_shapes=[
@@ -300,14 +320,15 @@
             pltpu.VMEM((levels, devices * slot, LANES), f32),
             pltpu.VMEM((levels, devices * slot, LANES), f32),
             pltpu.VMEM((levels, total, 3 * devices), jnp.bfloat16),
+            pltpu.VMEM((total, own * columns), f32),
             dma((4 + blocks,)),
-            dma(()), dma((3,)), dma(()), dma(()),
+            dma(()), dma(()), dma((devices,)),
             dma((levels,)), dma((levels,)),
         ],
         compiler_params=pltpu.CompilerParams(collective_id=0, has_side_effects=True),
         name="smooth_and_send",
     )(perturbation, vertical, kappa, sea_mask, sweeps)
-    return result.reshape(total, own, columns)
+    return result
 
 
 def solution(mesh):

time: 74.9 us -> 74.5 us (level)
    reshape x1 -> x0, local copies, waits for them, and re-layouts: 1.68 us -> none  [per_device(): return result.reshape(total, own, columns)]
    unnamed x0 -> x1, local copies, waits for them, and re-layouts: none -> 0.97 us
where the time goes in v4:
time: 74.5 us; the launch traced here: 74.4 us
  Pallas kernels  73.4 us (99%)
  local copies, waits for them, and re-layouts  0.97 us (1%)
    pallas_call x1, Pallas kernels, per_device(): pl.pallas_call(functools.partial(kernel, devices, levels, rows), out_shap...  73.4 us

profile of v4, /device:TPU:583, one launch (start us, length us, event | category | flops | bytes accessed | tf_op | source)
XLA Modules:
  0.0 74.4 jit_solution(3807840385133009996)
XLA Ops:
  0.0 73.4 %smooth_and_send.1 = f32[128,4,512]{2,1,0:T(4,128)S(1)} custom-call(f32[4,128,512]{2,1,0:T(8,128)} %pert.1, f32[128,128]{1,0:T(8,128)} %vert.1, f32[4,512]{1,0:T(4,128)} %kappa.1, s32[4,512]{1,0:T(4,128)} %mask.1, s32[3]{0:T(128)} %sweeps.1), custom_call_target="tpu_custom_call" | custom-call | tf_op jit(solution)/shard_map/smooth_and_send/pallas_call | solution.py:305
  73.4 1.0 %copy.7 = f32[128,4,512]{2,1,0:T(4,128)} copy(f32[128,4,512]{2,1,0:T(4,128)S(1)} %smooth_and_send.1) | data formatting | bytes 2097152

commit v5 on v4

--- a/solution.py
+++ b/solution.py
@@ -16,7 +16,7 @@
 
 def kernel(devices, levels, rows, pert, vert, kappa, mask, sweeps, out,
            xin, vin, kin, min_, cnt, kb, coef, xi, src, sb, rb, lhs, acc,
-           load_sem, one_send, two_send, block_recv, send_sem, recv_sem):
+           load_sem, one_send, one_recv, two_send, two_recv, send_sem, recv_sem):
     chips = devices // 2
     steps = rows // SUBS
     blocks = pert.shape[2] // LANES
@@ -70,7 +70,7 @@
             pert.at[:, :, pl.ds(cb * LANES, LANES)], xin.at[:, cb], load_sem.at[4 + cb]))
     for load in loads[:2]:
         load.start()
-    near = [at(s * d, c) for d in range(1, reach + 1) for s in (1, -1) for c in (core, 1 - core)] + [partner]
+    near = [at(s * d, c) for d in range(reach, 0, -1) for s in (1, -1) for c in (core, 1 - core)] + [partner]
     for device in near:
         pl.semaphore_signal(barrier, inc=1, device_id={"gx": device}, device_id_type=MESH)
 
@@ -88,17 +88,21 @@
 
     pl.semaphore_wait(barrier, len(near))
 
-    def give(block, device, ssem):
-        pltpu.make_async_remote_copy(
-            src_ref=kb.at[block], dst_ref=kb.at[block], send_sem=ssem,
-            recv_sem=block_recv.at[block],
-            device_id={"gx": device}, device_id_type=MESH).start()
-
-    for d in range(reach, 0, -1):
+    def give(block, device, ssem, rsem):
+        copy = pltpu.make_async_remote_copy(
+            src_ref=kb.at[block], dst_ref=kb.at[block], send_sem=ssem, recv_sem=rsem,
+            device_id={"gx": device}, device_id_type=MESH)
+        copy.start()
+
+    give(me, at(reach, core), one_send, one_recv.at[0])
+    give(me, at(-reach, core), one_send, one_recv.at[1])
+    give(me, at(reach, 1 - core), one_send, one_recv.at[2])
+    give(me, at(-reach, 1 - core), one_send, one_recv.at[2])
+    for d in range(reach - 1, 0, -1):
         for c in (core, 1 - core):
-            give(me, at(d, c), one_send)
-            give(me, at(-d, c), one_send)
-    give(me, partner, one_send)
+            give(me, at(d, c), one_send, one_recv.at[2])
+            give(me, at(-d, c), one_send, one_recv.at[2])
+    give(me, partner, one_send, one_recv.at[2])
 
     for load in loads[2:]:
         load.wait()
@@ -115,28 +119,17 @@
         lhs[c] = (jnp.dot(vh, high, preferred_element_type=jnp.float32)
                   + jnp.dot(vl, low, preferred_element_type=jnp.float32)).astype(jnp.bfloat16)
 
-    def sent(blocks_, sem):
+    def arrived(blocks_, sem):
         pltpu.make_async_copy(kb.at[pl.ds(0, blocks_)], kb.at[pl.ds(0, blocks_)], sem).wait()
 
-    def arrived(block):
-        pltpu.make_async_copy(kb.at[block], kb.at[block], block_recv.at[block]).wait()
-
-    below, above = at(-reach, core), at(reach, core)
-    arrived(below)
+    arrived(1, one_recv.at[0])
     for d in range(reach, 0, -1):
         for c in (core, 1 - core):
-            give(below, at(d, c), two_send)
-    arrived(above)
+            give(at(-reach, core), at(d, c), two_send, two_recv)
+    arrived(1, one_recv.at[1])
     for d in range(reach - 1, 0, -1):
         for c in (core, 1 - core):
-            give(above, at(-d, c), two_send)
-
-    def others_arrived(start, stop):
-        @pl.loop(start, stop)
-        def _(j):
-            @pl.when((j != me) & (j != below) & (j != above))
-            def _():
-                arrived(j)
+            give(at(reach, core), at(-d, c), two_send, two_recv)
 
     @pl.loop(0, levels)
     def _(l):
@@ -236,7 +229,8 @@
         for j in wanted:
             send(l, sb.at[l], jnp.where(me == j, devices - 1, j))
 
-    others_arrived(0, devices)
+    arrived(4 * reach - 1, one_recv.at[2])
+    arrived(4 * reach - 2, two_recv)
     couple(steps)
 
     @pl.loop(0, levels)
@@ -288,8 +282,8 @@
     def _(l):
         pltpu.make_async_copy(sb.at[l, others], sb.at[l, others], send_sem.at[l]).wait()
 
-    sent(4 * reach + 1, one_send)
-    sent(4 * reach - 2, two_send)
+    arrived(4 * reach + 1, one_send)
+    arrived(4 * reach - 2, two_send)
 
 
 def per_device(perturbation, vertical, kappa, sea_mask, sweeps):
@@ -322,7 +316,7 @@
             pltpu.VMEM((levels, total, 3 * devices), jnp.bfloat16),
             pltpu.VMEM((total, own * columns), f32),
             dma((4 + blocks,)),
-            dma(()), dma(()), dma((devices,)),
+            dma(()), dma((3,)), dma(()), dma(()),
             dma((levels,)), dma((levels,)),
         ],
         compiler_params=pltpu.CompilerParams(collective_id=0, has_side_effects=True),

time: 74.5 us -> 73.9 us (level)
  no operation moved by 1% of the time
where the time goes in v5:
time: 73.9 us; the launch traced here: 73.8 us
  Pallas kernels  72.8 us (99%)
  local copies, waits for them, and re-layouts  0.97 us (1%)
    pallas_call x1, Pallas kernels, per_device(): pl.pallas_call(functools.partial(kernel, devices, levels, rows), out_shap...  72.8 us

profile of v5, /device:TPU:583, one launch (start us, length us, event | category | flops | bytes accessed | tf_op | source)
XLA Modules:
  0.0 73.8 jit_solution(3226378151128332168)
XLA Ops:
  0.0 72.8 %smooth_and_send.1 = f32[128,4,512]{2,1,0:T(4,128)S(1)} custom-call(f32[4,128,512]{2,1,0:T(8,128)} %pert.1, f32[128,128]{1,0:T(8,128)} %vert.1, f32[4,512]{1,0:T(4,128)} %kappa.1, s32[4,512]{1,0:T(4,128)} %mask.1, s32[3]{0:T(128)} %sweeps.1), custom_call_target="tpu_custom_call" | custom-call | tf_op jit(solution)/shard_map/smooth_and_send/pallas_call | solution.py:299
  72.8 1.0 %copy.7 = f32[128,4,512]{2,1,0:T(4,128)} copy(f32[128,4,512]{2,1,0:T(4,128)S(1)} %smooth_and_send.1) | data formatting | bytes 2097152

commit v6 on v5

--- a/solution.py
+++ b/solution.py
@@ -202,10 +202,8 @@
                     src[t, cb] = u[t, cb] * coef[4, t, cb]
             most = jnp.full((SUBS, LANES), cnt[section], jnp.int32)
 
-            @pl.loop(0, SWEEP_LEAST, step=2)
-            def _(i):
-                sweep(u, count, 0, None)
-                sweep(u, count, 2, None)
+            for i in range(SWEEP_LEAST):
+                sweep(u, count, 2 * i, None)
 
             @pl.loop(SWEEP_LEAST, SWEEP_MOST, step=2)
             def _(i):

time: 73.9 us -> 73.8 us (level)
  no operation moved by 1% of the time
where the time goes in v6:
time: 73.8 us; the launch traced here: 73.7 us
  Pallas kernels  72.7 us (99%)
  local copies, waits for them, and re-layouts  0.97 us (1%)
    pallas_call x1, Pallas kernels, per_device(): pl.pallas_call(functools.partial(kernel, devices, levels, rows), out_shap...  72.7 us

profile of v6, /device:TPU:583, one launch (start us, length us, event | category | flops | bytes accessed | tf_op | source)
XLA Modules:
  0.0 73.7 jit_solution(7871956565922093708)
XLA Ops:
  0.0 72.7 %smooth_and_send.1 = f32[128,4,512]{2,1,0:T(4,128)S(1)} custom-call(f32[4,128,512]{2,1,0:T(8,128)} %pert.1, f32[128,128]{1,0:T(8,128)} %vert.1, f32[4,512]{1,0:T(4,128)} %kappa.1, s32[4,512]{1,0:T(4,128)} %mask.1, s32[3]{0:T(128)} %sweeps.1), custom_call_target="tpu_custom_call" | custom-call | tf_op jit(solution)/shard_map/smooth_and_send/pallas_call | solution.py:297
  72.7 1.0 %copy.7 = f32[128,4,512]{2,1,0:T(4,128)} copy(f32[128,4,512]{2,1,0:T(4,128)S(1)} %smooth_and_send.1) | data formatting | bytes 2097152
